TPU v7x, 32 devices: a whole 2x2x4 slice. The times are simulated.
32 devices in a mesh: seq: 16 (over z, x, core), head: 2 (over y).
Axes of the slice: x: 2, y: 2, z: 4, core: 2. Of those that a mesh axis runs over, the one named last changes fastest.
Arguments:
- query: bfloat16 [1, 4096, 2048], P(None, 'seq', 'head'), may hold values from -210 to 210
- keys: bfloat16 [1, 4096, 512], P(None, 'seq', 'head'), may hold values from -7 to 7
- values: bfloat16 [1, 4096, 512], P(None, 'seq', 'head'), may hold values from -6 to 6
- grad_out: bfloat16 [1, 4096, 2048], P(None, 'seq', 'head'), may hold values from -6 to 6
- global_offset: int32 [1, 64], replicated, may hold values from 0 to 255, as said below
- owner: int32 [16], replicated, may hold values from 0 to 15, each once
- block_lists: int32 [1, 32, 3], P(None, 'seq'), may hold values from 0 to 31, as said below
Outputs:
- grad_query: bfloat16 [1, 4096, 2048], P(None, 'seq', 'head')
- grad_keys: bfloat16 [1, 4096, 512], P(None, 'seq', 'head')
- grad_values: bfloat16 [1, 4096, 512], P(None, 'seq', 'head')
Inputs may be any that keep to these rules, and one draw needn't show every extreme that they name: `block_lists`: row b of each layer lists b first, then 3 - 1 other distinct blocks within 2 blocks of b. `global_offset`: distinct within a layer. `owner`: each sequence shard appears once.
All inputs are finite; a program needn't handle non-finite values.
Results may differ from a plain program's by a relative error of at most 0.02.
Values may be sent and summed in bfloat16 or wider, within the bound.
A program may use at most 64 MiB of HBM per device.

v0:
```python
import jax
import jax.numpy as jnp
from jax import lax
from jax.sharding import PartitionSpec as P

HQ = 16
HK = 4
DH = 128
BLOCK = 128
REACH = 2
G = 64


def padded(block, sides, width):
    for axis, dim in sides:
        count = lax.axis_size(axis)
        forward = [(i, i + 1) for i in range(count - 1)]
        backward = [(target, source) for source, target in forward]
        low = lax.ppermute(
            lax.slice_in_dim(block, block.shape[dim] - width, None, axis=dim), axis, forward
        )
        high = lax.ppermute(lax.slice_in_dim(block, 0, width, axis=dim), axis, backward)
        block = jnp.concatenate([low, block, high], axis=dim)
    return block


def spread_2(array, axis, root):
    mine = lax.axis_index(axis) == root
    return lax.psum(jnp.where(mine, array, jnp.zeros_like(array)), axis)


def passed_along(value, axis, steps):
    count = lax.axis_size(axis)
    first, last = (max(0, -steps), min(count, count - steps))
    return lax.ppermute(value, axis, [(source, source + steps) for source in range(first, last)])


def scores(q_block, k_rows):
    return jnp.einsum(
        "tcgd,scd->cgts", q_block, k_rows, preferred_element_type=jnp.float32
    ) * DH ** (-0.5)


def backward(q_block, g_block, k_rows, v_rows, attn_probs, out_dot):
    attn_half = attn_probs.astype(jnp.bfloat16)
    grad_probs = jnp.einsum("tcgd,scd->cgts", g_block, v_rows, preferred_element_type=jnp.float32)
    grad_logits = (attn_probs * (grad_probs - out_dot[..., None])).astype(jnp.bfloat16)
    grad_q = jnp.einsum(
        "cgts,scd->tcgd", grad_logits, k_rows, preferred_element_type=jnp.float32
    ) * DH ** (-0.5)
    grad_k = jnp.einsum(
        "cgts,tcgd->scd", grad_logits, q_block, preferred_element_type=jnp.float32
    ) * DH ** (-0.5)
    grad_v = jnp.einsum("cgts,tcgd->scd", attn_half, g_block, preferred_element_type=jnp.float32)
    return (grad_q, grad_k, grad_v)


def attend(q_block, g_block, k_rows, v_rows):
    logits = scores(q_block, k_rows)
    top_logit = jnp.max(logits, axis=-1, keepdims=True)
    log_total = top_logit + jnp.log(jnp.sum(jnp.exp(logits - top_logit), axis=-1, keepdims=True))
    attn_probs = jnp.exp(logits - log_total)
    attn_half = attn_probs.astype(jnp.bfloat16)
    output = jnp.einsum(
        "cgts,scd->tcgd", attn_half, v_rows, preferred_element_type=jnp.float32
    ).astype(jnp.bfloat16)
    out_dot = jnp.einsum("tcgd,tcgd->cgt", g_block, output, preferred_element_type=jnp.float32)
    grad_q, grad_k, grad_v = backward(q_block, g_block, k_rows, v_rows, attn_probs, out_dot)
    return (grad_q, grad_k, grad_v, log_total[..., 0], out_dot)


def local(query, keys, values, grad_out, global_offset, owner, block_lists):
    row_count = query.shape[1]
    kv_width = keys.shape[2]
    heads_kv = kv_width // DH
    group_size = HQ // HK
    block_count = row_count // BLOCK
    listed = block_lists.shape[2]
    window_len = listed * BLOCK
    margin = REACH * BLOCK
    shard_index = lax.axis_index("seq")
    first_block = shard_index * block_count
    kv_pair = jnp.stack([keys[0], values[0]])
    widened = padded(kv_pair, (("seq", 1),), margin)
    picked = jnp.take(kv_pair, global_offset[0], axis=1)
    shared = spread_2(picked, "seq", owner[0])
    blocks = widened.reshape(2, block_count + 2 * REACH, BLOCK, heads_kv, DH)
    local_idx = block_lists[0] - first_block + REACH
    window = blocks[:, local_idx].reshape(2, block_count, window_len, heads_kv, DH)
    global_rows = jnp.broadcast_to(
        shared.reshape(2, 1, G, heads_kv, DH), (2, block_count, G, heads_kv, DH)
    )
    key_rows = jnp.concatenate([window, global_rows], axis=2)
    q_blocks = query[0].reshape(block_count, BLOCK, heads_kv, group_size, DH)
    g_blocks = grad_out[0].reshape(block_count, BLOCK, heads_kv, group_size, DH)
    grad_q, grad_k, grad_v, log_total, out_dot = jax.vmap(attend)(
        q_blocks, g_blocks, key_rows[0], key_rows[1]
    )
    grads_q = [grad_q.astype(jnp.bfloat16).reshape(row_count, -1)]
    partial_value = jnp.stack([grad_k[:, :window_len], grad_v[:, :window_len]]).reshape(
        2, block_count * listed, BLOCK, kv_width
    )
    spread = (
        jnp.zeros((2, block_count + 2 * REACH, BLOCK, kv_width), jnp.float32)
        .at[:, local_idx.reshape(-1)]
        .add(partial_value)
    )
    spread = spread.reshape(2, row_count + 2 * margin, kv_width)
    own_sums = spread[:, margin : margin + row_count]
    from_next = passed_along(spread[:, :margin], "seq", -1)
    from_prev = passed_along(spread[:, margin + row_count :], "seq", 1)
    own_sums = own_sums.at[:, :margin].add(from_prev).at[:, row_count - margin :].add(from_next)
    global_part = jnp.stack(
        [jnp.sum(grad_k[:, window_len:], axis=0), jnp.sum(grad_v[:, window_len:], axis=0)]
    )
    global_part = global_part.reshape(2, G, kv_width)
    owner_flag = (owner[0] == shard_index).astype(jnp.float32)
    share = lax.psum_scatter(global_part.reshape(-1), "seq", scatter_dimension=0, tiled=True)
    global_total = lax.all_gather(share, "seq", axis=0, tiled=True).reshape(2, G, kv_width)
    own_sums = own_sums.at[:, global_offset[0]].add(global_total * owner_flag)
    owned = [own_sums]
    grad_keys = jnp.stack([sums[0] for sums in owned]).astype(jnp.bfloat16)
    grad_values = jnp.stack([sums[1] for sums in owned]).astype(jnp.bfloat16)
    return (jnp.stack(grads_q), grad_keys, grad_values)


def solution(mesh):
    return jax.shard_map(
        local,
        mesh=mesh,
        in_specs=(
            P(None, "seq", "head"),
            P(None, "seq", "head"),
            P(None, "seq", "head"),
            P(None, "seq", "head"),
            P(),
            P(),
            P(None, "seq", None),
        ),
        out_specs=(P(None, "seq", "head"), P(None, "seq", "head"), P(None, "seq", "head")),
        check_vma=False,
    )
```

profile of v0, /device:TPU:0, one launch (start us, length us, event | category | flops | bytes accessed | tf_op | source)
XLA Modules:
  0.0 249.0 jit_solution(18314176029845374509)
XLA Ops:
  7.2 0.0 all-reduce.4.cloned.1.call-start
  7.2 1.1 copy.93
  8.3 1.1 copy.94
  9.4 0.6 pad_maximum_fusion.2
  10.1 2.4 collective-permute-start
  12.5 1.3 collective-permute-start.1
  13.8 0.7 fusion.28
  14.4 0.7 compare_and_fusion
  15.1 0.7 gather_fusion.1
  16.5 0.2 fusion.27
  16.7 0.6 copy.98
  17.4 0.0 all-reduce.6.cloned.1.call-start
  17.4 0.7 compare_select_fusion
  18.1 0.1 reshape.196
  18.8 1.4 reshape_squeeze.6
  20.2 1.4 reshape_squeeze.7
  21.7 0.1 add.121
  21.7 0.1 add.122
  21.8 0.6 dynamic-slice.10
  23.1 1.3 pad_maximum_fusion
  24.4 0.5 reshape.234
  24.9 0.2 copy.96
  25.1 0.7 gather_fusion
  25.8 0.1 copy.97
  25.9 82.3 %all-reduce.4.cloned.1.call-done = bf16[2,64,2,128]{3,1,2,0:T(8,128)(2,1)} async-done(((bf16[2,64,2,128]{3,1,2,0:T(8,128)(2,1)}), bf16[2,64,2,128]{3,1,2,0:T(8,128)(2,1)}) %all-reduce.4.cloned.1.call-update) | async-done | bytes 65552 | tf_op jit(solution)/shard_map/psum | solution.py:29
  108.2 0.9 broadcast_in_dim.33
  109.1 0.7 bitcast_reduce_fusion
  109.7 0.6 fusion.3
  110.4 1.8 fusion.10
  112.2 0.7 convolution_bitcast_fusion
  112.9 0.9 slice.96
  113.9 1.7 copy.121
  115.6 0.9 multiply_reduce_fusion
  116.4 0.1 copy.122
  116.5 3.1 %fusion.1 = bf16[2,2,4,128,448]{3,4,2,1,0:T(8,128)(2,1)S(1)} fusion(f32[2,2,448,128,4]{3,2,4,1,0:T(8,128)} %copy-done, f32[2,2,4,128]{3,2,1,0:T(4,128)S(1)} %copy.122, f32[2,2,4,128]{3,2,1,0:T(4,128)S(1)} %bitcast.113, bf16[2,128,2,4,128]{4,3,2,1,0:T(4,128)(2,1)S(1)} %reshape_squeeze.7, bf16[2,2,64,2,128]{4,2,3,1,0:T(8,128)(2,1)S(1)} %broadcast_in_dim.33, ...), kind=kOutput, calls=%fused_computation.6 | convolution fusion | flops 240386048 | bytes 6963200 | tf_op jit(solution)/shard_map/vmap(tcgd,scd->cgts)/dot_general | solution.py:46
  119.6 0.6 fusion.7
  120.3 0.1 slice.95
  120.4 1.3 fusion.11
  121.7 0.8 copy.110
  122.5 0.6 copy.105
  123.1 0.6 stack.23
  123.7 0.6 copy.103
  124.3 0.6 stack.22
  125.0 0.1 maximum_bitcast_fusion
  125.1 0.1 copy.106
  125.2 0.1 broadcast_in_dim.34
  125.3 1.8 scatter_fusion
  127.2 0.2 fusion.36
  127.4 0.4 copy.128
  127.8 2.0 collective-permute-start.2
  129.8 0.4 copy.129
  130.2 1.3 collective-permute-start.3
  131.5 0.3 copy.101
  131.8 1.2 stack_reshape.3
  133.0 79.5 %all-reduce.6.cloned.1.call-done = f32[32768]{0:T(1024)} async-done(((f32[32768]{0:T(1024)}), f32[32768]{0:T(1024)}) %all-reduce.6.cloned.1.call-update) | async-done | bytes 131088
  212.5 0.7 dynamic-slice.11
  213.2 22.3 %all_gather.3 = f32[32768]{0:T(1024)S(1)} all-gather(f32[2048]{0:T(1024)S(1)} %dynamic-slice.11), channel_id=1, replica_groups=mesh['seq'=16,'head'=2] {'seq'}, dimensions={0}, use_global_device_ids=true | all-gather | bytes 139264 | tf_op jit(solution)/shard_map/all_gather | solution.py:119
  235.6 0.1 copy.111
  235.7 1.7 fusion.12
  237.4 2.9 %scatter_fusion.1 = f32[2,256,256]{2,0,1:T(2,128)S(1)} fusion(f32[2,256,256]{2,0,1:T(2,128)S(1)} %fusion.12, s32[64]{0:T(128)S(1)} %fusion.28, f32[64,2,256]{2,1,0:T(2,128)S(1)} %copy.111), kind=kCustom, calls=%fused_computation.3 | custom fusion | flops 32768 | bytes 393472 | tf_op jit(solution)/shard_map/scatter-add | solution.py:120
  240.2 0.2 convert.4
  240.4 0.4 fusion.37
  240.8 0.7 copy.112
  241.5 0.7 copy.113
  (24 shorter events, 0.2 us)
Async XLA Ops:
  7.2 14.7 %copy-start.3 = (u32[32]{0:T(128)S(1)}, u32[32]{0:T(128)}, u32[]{:S(2)}) copy-start(u32[32]{0:T(128)} %constant.115) | copy-start | bytes 388
  7.2 101.0 %all-reduce.4.cloned.1.call-start = ((), (), s32[]{:S(2)}) async-start(), calls=%async_computation | async-start | bytes 131072 | tf_op jit(solution)/shard_map/psum | solution.py:29
  10.1 13.0 %collective-permute-start = (bf16[2,256,256]{2,0,1:T(2,128)(2,1)S(1)}, bf16[2,256,256]{2,0,1:T(2,128)(2,1)S(1)}, u32[]{:S(2)}, u32[]{:S(2)}) collective-permute-start(bf16[2,256,256]{2,0,1:T(2,128)(2,1)S(1)} %pad_maximum_fusion.2), channel_id=1, source_target_pairs={{0,2},{2,4},{4,6},{6,8},{8,10},{10,12},{12,14},{14,16},{16,18},{18... | collective-permute-start | bytes 786440 | tf_op jit(solution)/shard_map/ppermute | solution.py:19
  12.5 10.6 %collective-permute-start.1 = (bf16[2,256,256]{2,0,1:T(2,128)(2,1)S(1)}, bf16[2,256,256]{2,0,1:T(2,128)(2,1)S(1)}, u32[]{:S(2)}, u32[]{:S(2)}) collective-permute-start(bf16[2,256,256]{2,0,1:T(2,128)(2,1)S(1)} %pad_maximum_fusion.2), channel_id=1, source_target_pairs={{2,0},{4,2},{6,4},{8,6},{10,8},{12,10},{14,12},{16,14},{18,16},{20... | collective-permute-start | bytes 786440 | tf_op jit(solution)/shard_map/ppermute | solution.py:22
  17.4 195.2 %all-reduce.6.cloned.1.call-start = ((), (), s32[]{:S(2)}) async-start(), calls=%async_computation.1 | async-start | bytes 262144
  109.7 2.5 copy-start
  120.3 2.2 copy-start.1
  127.2 4.4 %copy-start.2 = (bf16[2,128,2,4,128]{1,4,3,2,0:T(8,128)(2,1)S(1)}, bf16[2,128,2,4,128]{1,4,3,2,0:T(8,128)(2,1)}, u32[]{:S(2)}) copy-start(bf16[2,128,2,4,128]{1,4,3,2,0:T(8,128)(2,1)} %fusion.11) | copy-start | bytes 1572868
  127.8 107.9 %collective-permute-start.2 = (f32[2,256,256]{2,0,1:T(2,128)S(1)}, f32[2,256,256]{2,0,1:T(2,128)S(1)}, u32[]{:S(2)}, u32[]{:S(2)}) collective-permute-start(f32[2,256,256]{2,0,1:T(2,128)S(1)} %copy.128), channel_id=1, source_target_pairs={{0,2},{2,4},{4,6},{6,8},{8,10},{10,12},{12,14},{14,16},{16,18},{18... | collective-permute-start | bytes 1572872 | tf_op jit(solution)/shard_map/ppermute | solution.py:35
  130.2 105.5 %collective-permute-start.3 = (f32[2,256,256]{2,0,1:T(2,128)S(1)}, f32[2,256,256]{2,0,1:T(2,128)}, u32[]{:S(2)}, u32[]{:S(2)}) collective-permute-start(f32[2,256,256]{2,0,1:T(2,128)S(1)} %copy.129), channel_id=1, source_target_pairs={{2,0},{4,2},{6,4},{8,6},{10,8},{12,10},{14,12},{16,14},{18,16},{20... | collective-permute-start | bytes 1572872 | tf_op jit(solution)/shard_map/ppermute | solution.py:35
Sparse Core Ops, SparseCore 0:
  17.5 90.6 all-reduce.3
  122.6 89.8 all-reduce.5
where the time goes:
time: 250 us; the launch traced here: 249 us
  waiting for transfers between devices  162 us (65%)
  blocking collectives  22.3 us (9%)
  local copies, waits for them, and re-layouts  20.8 us (8%)
  between operations  16.4 us (7%)
  other arithmetic  12.2 us (5%)
  matrix products  8.23 us (3%)
  starting transfers between devices  7.11 us (3%)
    psum x1, waiting for transfers between devices, spread_2(): return lax.psum(jnp.where(mine, array, jnp.zeros_like(array)), axis)  82.3 us
    unnamed x3, waiting for transfers between devices  79.5 us
    all_gather x1, blocking collectives, local(): lax.all_gather(share, 'seq', axis=0, tiled=True).reshape(2, G, kv_width)  22.3 us
    unnamed x17, local copies, waits for them, and re-layouts  7.34 us
  transfers between devices with their start and end apart: 6, of which 2 were waited for; matrix products, arithmetic and copies ran while one was open for 7% of the time, Pallas kernels for 0%

commit v1 on v0

--- a/solution.py
+++ b/solution.py
@@ -26,7 +26,7 @@
 
 def spread_2(array, axis, root):
     mine = lax.axis_index(axis) == root
-    return lax.psum(jnp.where(mine, array, jnp.zeros_like(array)), axis)
+    return jnp.sum(lax.all_gather(jnp.where(mine, array, jnp.zeros_like(array)), axis), axis=0)
 
 
 def passed_along(value, axis, steps):

time: 250 us -> 194 us (0.78)
  waiting for transfers between devices: 162 us -> 105 us
    psum x1 -> x0, waiting for transfers between devices: 82.3 us -> none  [spread_2(): return lax.psum(jnp.where(mine, array, jnp.zeros_like(array)), axis)]
    all_gather x0 -> x1, waiting for transfers between devices: none -> 28.6 us  [spread_2(): lax.all_gather(jnp.where(mine, array, jnp.zeros_like(array)), axis)]
    unnamed x3, waiting for transfers between devices: 79.5 us -> 76.8 us
  transfers between devices with their start and end apart: 6 -> 6, of which waited for: 2 -> 2; matrix products, arithmetic and copies ran while one was open for 7% -> 8% of each run, Pallas kernels for 0% -> 0%
where the time goes in v1:
time: 194 us; the launch traced here: 193 us
  waiting for transfers between devices  105 us (54%)
  blocking collectives  22.3 us (11%)
  local copies, waits for them, and re-layouts  19.9 us (10%)
  between operations  16.4 us (8%)
  other arithmetic  13.6 us (7%)
  matrix products  8.23 us (4%)
  starting transfers between devices  7.23 us (4%)
    unnamed x3, waiting for transfers between devices  76.8 us
    all_gather x1, waiting for transfers between devices, spread_2(): lax.all_gather(jnp.where(mine, array, jnp.zeros_like(array)), axis)  28.6 us
    all_gather x1, blocking collectives, local(): lax.all_gather(share, 'seq', axis=0, tiled=True).reshape(2, G, kv_width)  22.3 us
    unnamed x17, local copies, waits for them, and re-layouts  7.34 us
  transfers between devices with their start and end apart: 6, of which 2 were waited for; matrix products, arithmetic and copies ran while one was open for 8% of the time, Pallas kernels for 0%

profile of v1, /device:TPU:0, one launch (start us, length us, event | category | flops | bytes accessed | tf_op | source)
XLA Modules:
  0.0 193.2 jit_solution(15997842597610727909)
XLA Ops:
  7.2 0.0 all-gather.2.cloned.1.call-start
  7.2 0.7 fusion.27
  7.9 0.7 compare_and_fusion
  8.5 1.1 copy.95
  9.7 1.1 copy.96
  10.8 0.6 pad_maximum_fusion.2
  11.4 0.7 gather_fusion.1
  12.8 0.2 broadcast_select_fusion.1
  12.9 0.6 copy.100
  13.6 0.0 all-reduce.3.cloned.1.call-start
  13.6 2.4 %collective-permute-start = (bf16[2,256,256]{2,0,1:T(2,128)(2,1)S(1)}, bf16[2,256,256]{2,0,1:T(2,128)(2,1)S(1)}, u32[]{:S(2)}, u32[]{:S(2)}) collective-permute-start(bf16[2,256,256]{2,0,1:T(2,128)(2,1)S(1)} %pad_maximum_fusion.2), channel_id=1, source_target_pairs={{0,2},{2,4},{4,6},{6,8},{8,10},{10,12},{12,14},{14,16},{16,18},{18... | collective-permute-start | bytes 786440 | tf_op jit(solution)/shard_map/ppermute | solution.py:19
  16.1 1.3 collective-permute-start.1
  17.4 0.7 compare_select_fusion
  18.0 0.1 reshape.206
  18.8 1.4 reshape_squeeze.6
  20.2 1.4 reshape_squeeze.7
  21.6 0.1 add.119
  21.7 0.1 add.120
  21.8 0.6 dynamic-slice.10
  23.1 1.3 pad_maximum_fusion
  24.4 0.5 reshape.244
  24.9 0.2 copy.98
  25.0 0.7 gather_fusion
  25.7 0.1 copy.99
  25.8 28.6 %all-gather.2.cloned.1.call-done = bf16[16,2,64,256]{3,2,1,0:T(8,128)(2,1)} async-done(((bf16[1,2,64,256]{3,2,1,0:T(8,128)(2,1)}), bf16[16,2,64,256]{3,2,1,0:T(8,128)(2,1)}) %all-gather.2.cloned.1.call-update) | async-done | bytes 1048592 | tf_op jit(solution)/shard_map/all_gather | solution.py:29
  54.4 1.4 reduce_sum.39
  55.8 0.7 bitcast_reduce_fusion
  56.5 0.6 fusion.3
  57.2 1.8 fusion.10
  59.0 0.7 convolution_bitcast_fusion
  59.7 0.9 slice.96
  60.7 1.7 copy.126
  62.3 0.9 multiply_reduce_fusion
  63.2 0.1 copy.127
  63.3 3.1 %fusion.1 = bf16[2,2,4,128,448]{3,4,2,1,0:T(8,128)(2,1)S(1)} fusion(f32[2,2,448,128,4]{3,2,4,1,0:T(8,128)} %copy-done, f32[2,2,4,128]{3,2,1,0:T(4,128)S(1)} %copy.127, f32[2,2,4,128]{3,2,1,0:T(4,128)S(1)} %bitcast.120, bf16[2,128,2,4,128]{4,3,2,1,0:T(4,128)(2,1)S(1)} %reshape_squeeze.7, bf16[2,2,64,2,128]{4,2,3,1,0:T(8,128)(2,1)S(1)} %broadcast_in_dim.33, ...), kind=kOutput, calls=%fused_computation.6 | convolution fusion | flops 240386048 | bytes 6963200 | tf_op jit(solution)/shard_map/vmap(tcgd,scd->cgts)/dot_general | solution.py:46
  66.4 0.6 fusion.7
  67.1 0.1 slice.95
  67.1 1.3 fusion.11
  68.5 0.8 copy.115
  69.3 0.6 copy.110
  69.9 0.6 stack.23
  70.5 0.6 copy.108
  71.1 0.6 stack.22
  71.8 0.1 maximum_bitcast_fusion
  71.9 0.1 copy.111
  72.0 0.1 broadcast_in_dim.34
  72.1 1.8 scatter_fusion
  74.0 0.2 fusion.35
  74.1 0.4 copy.136
  74.5 2.2 %collective-permute-start.2 = (f32[2,256,256]{2,0,1:T(2,128)S(1)}, f32[2,256,256]{2,0,1:T(2,128)S(1)}, u32[]{:S(2)}, u32[]{:S(2)}) collective-permute-start(f32[2,256,256]{2,0,1:T(2,128)S(1)} %copy.136), channel_id=1, source_target_pairs={{0,2},{2,4},{4,6},{6,8},{8,10},{10,12},{12,14},{14,16},{16,18},{18... | collective-permute-start | bytes 1572872 | tf_op jit(solution)/shard_map/ppermute | solution.py:35
  76.7 0.4 copy.137
  77.1 1.3 collective-permute-start.3
  78.4 0.3 copy.106
  78.8 1.2 stack_reshape.3
  79.9 76.8 %all-reduce.3.cloned.1.call-done = f32[32768]{0:T(1024)} async-done(((f32[32768]{0:T(1024)}), f32[32768]{0:T(1024)}) %all-reduce.3.cloned.1.call-update) | async-done | bytes 131088
  156.7 0.7 dynamic-slice.11
  157.4 22.3 %all_gather.8 = f32[32768]{0:T(1024)S(1)} all-gather(f32[2048]{0:T(1024)S(1)} %dynamic-slice.11), channel_id=1, replica_groups=mesh['seq'=16,'head'=2] {'seq'}, dimensions={0}, use_global_device_ids=true | all-gather | bytes 139264 | tf_op jit(solution)/shard_map/all_gather | solution.py:119
  179.8 0.1 copy.116
  179.9 1.7 fusion.12
  181.6 2.9 %scatter_fusion.1 = f32[2,256,256]{2,0,1:T(2,128)S(1)} fusion(f32[2,256,256]{2,0,1:T(2,128)S(1)} %fusion.12, s32[64]{0:T(128)S(1)} %fusion.27, f32[64,2,256]{2,1,0:T(2,128)S(1)} %copy.116), kind=kCustom, calls=%fused_computation.3 | custom fusion | flops 32768 | bytes 393472 | tf_op jit(solution)/shard_map/scatter-add | solution.py:120
  184.4 0.2 convert.5
  184.6 0.4 fusion.36
  185.0 0.7 copy.117
  185.7 0.7 copy.118
  (25 shorter events, 0.2 us)
Async XLA Ops:
  7.2 14.6 %copy-start.3 = (u32[32]{0:T(128)S(1)}, u32[32]{0:T(128)}, u32[]{:S(2)}) copy-start(u32[32]{0:T(128)} %constant.116) | copy-start | bytes 388
  7.2 47.2 %all-gather.2.cloned.1.call-start = ((), (), s32[]{:S(2)}) async-start(), calls=%async_computation | async-start | bytes 1114112 | tf_op jit(solution)/shard_map/all_gather | solution.py:29
  13.6 143.1 %all-reduce.3.cloned.1.call-start = ((), (), s32[]{:S(2)}) async-start(), calls=%async_computation.1 | async-start | bytes 262144
  13.6 9.4 %collective-permute-start = (bf16[2,256,256]{2,0,1:T(2,128)(2,1)S(1)}, bf16[2,256,256]{2,0,1:T(2,128)(2,1)S(1)}, u32[]{:S(2)}, u32[]{:S(2)}) collective-permute-start(bf16[2,256,256]{2,0,1:T(2,128)(2,1)S(1)} %pad_maximum_fusion.2), channel_id=1, source_target_pairs={{0,2},{2,4},{4,6},{6,8},{8,10},{10,12},{12,14},{14,16},{16,18},{18... | collective-permute-start | bytes 786440 | tf_op jit(solution)/shard_map/ppermute | solution.py:19
  16.1 7.0 %collective-permute-start.1 = (bf16[2,256,256]{2,0,1:T(2,128)(2,1)S(1)}, bf16[2,256,256]{2,0,1:T(2,128)(2,1)S(1)}, u32[]{:S(2)}, u32[]{:S(2)}) collective-permute-start(bf16[2,256,256]{2,0,1:T(2,128)(2,1)S(1)} %pad_maximum_fusion.2), channel_id=1, source_target_pairs={{2,0},{4,2},{6,4},{8,6},{10,8},{12,10},{14,12},{16,14},{18,16},{20... | collective-permute-start | bytes 786440 | tf_op jit(solution)/shard_map/ppermute | solution.py:22
  56.5 2.5 %copy-start = (f32[2,2,448,128,4]{3,2,4,1,0:T(8,128)}, f32[2,2,448,128,4]{3,2,4,1,0:T(8,128)S(1)}, u32[]{:S(2)}) copy-start(f32[2,2,448,128,4]{3,2,4,1,0:T(8,128)S(1)} %get-tuple-element.70) | copy-start | bytes 11010052
  67.1 2.2 %copy-start.1 = (f32[2,384,2,128]{3,1,2,0:T(8,128)S(1)}, f32[2,384,2,128]{3,1,2,0:T(8,128)}, u32[]{:S(2)}) copy-start(f32[2,384,2,128]{3,1,2,0:T(8,128)} %slice.96) | copy-start | bytes 2359300
  73.9 4.5 %copy-start.2 = (bf16[2,128,2,4,128]{1,4,3,2,0:T(8,128)(2,1)S(1)}, bf16[2,128,2,4,128]{1,4,3,2,0:T(8,128)(2,1)}, u32[]{:S(2)}) copy-start(bf16[2,128,2,4,128]{1,4,3,2,0:T(8,128)(2,1)} %fusion.11) | copy-start | bytes 1572868
  74.5 105.3 %collective-permute-start.2 = (f32[2,256,256]{2,0,1:T(2,128)S(1)}, f32[2,256,256]{2,0,1:T(2,128)S(1)}, u32[]{:S(2)}, u32[]{:S(2)}) collective-permute-start(f32[2,256,256]{2,0,1:T(2,128)S(1)} %copy.136), channel_id=1, source_target_pairs={{0,2},{2,4},{4,6},{6,8},{8,10},{10,12},{12,14},{14,16},{16,18},{18... | collective-permute-start | bytes 1572872 | tf_op jit(solution)/shard_map/ppermute | solution.py:35
  77.1 102.8 %collective-permute-start.3 = (f32[2,256,256]{2,0,1:T(2,128)S(1)}, f32[2,256,256]{2,0,1:T(2,128)}, u32[]{:S(2)}, u32[]{:S(2)}) collective-permute-start(f32[2,256,256]{2,0,1:T(2,128)S(1)} %copy.137), channel_id=1, source_target_pairs={{2,0},{4,2},{6,4},{8,6},{10,8},{12,10},{14,12},{16,14},{18,16},{20... | collective-permute-start | bytes 1572872 | tf_op jit(solution)/shard_map/ppermute | solution.py:35
Sparse Core Ops, SparseCore 0:
  13.7 40.6 all-gather.1
  69.4 87.3 all-reduce.2
